TPU v7x, 512 devices: a whole 4x4x16 slice. The times are simulated.
512 devices in a mesh: blk: 32 (over x, y, core), rhs: 16 (over z).
Axes of the slice: x: 4, y: 4, z: 16, core: 2. Of those that a mesh axis runs over, the one named last changes fastest.
Arguments:
- lower_coupling: bfloat16 [2, 2048, 4096], P(None, 'blk'), may hold values from -0.0625 to 0.0625
- upper_coupling: bfloat16 [2, 2048, 4096], P(None, 'blk'), may hold values from -0.0625 to 0.0625
- lower_inverse: bfloat16 [2, 2048, 2048], P(None, 'blk'), may hold values from -1 to 2
- upper_inverse: bfloat16 [2, 2048, 2048], P(None, 'blk'), may hold values from -1 to 2
- right_side: float32 [2, 2048, 16384], P(None, 'blk', 'rhs'), parts along dimension 2, may hold values from -6 to 6
Outputs:
- solution: float32 [2, 2048, 16384], P(None, 'blk', 'rhs'), parts along dimension 2
There are 16 independent parts, one for each index of `rhs`. A program takes and returns all parts, laid end to end along the dimension named above; an argument that names none is the same for every part. Nothing has to cross between parts.
All inputs are finite; a program needn't handle non-finite values.
Results may differ from a plain program's by a relative error of at most 0.0043.
Values may be sent and summed in bfloat16 or wider, within the bound.
A program may use at most 64 MiB of HBM per device.

v0:
```python
import jax
import jax.numpy as jnp
from jax import lax
from jax.sharding import Mesh
from jax.sharding import PartitionSpec as P

SEP = 2048
BLK = ("blk_0", "blk_1", "blk_2")


def from_everyone(array, axis):
    size = lax.axis_size(axis)
    return lax.all_to_all(
        jnp.broadcast_to(array[None], (size, *array.shape)), axis, 0, 0, tiled=True
    )


def joined_along(blocks, dim):
    blocks = jnp.moveaxis(blocks, 0, dim)
    shape = blocks.shape
    return blocks.reshape(*shape[:dim], shape[dim] * shape[dim + 1], *shape[dim + 2 :])


def whole_of(array, axes, dim):
    far, near = axes
    first = from_everyone(array, far)
    blocks = jnp.swapaxes(from_everyone(first, near), 0, 1)
    return joined_along(blocks.reshape(-1, *array.shape), dim)


def sweep(pending, coupling, inverse, ascending):
    total_blocks = pending.shape[0]
    row_count = pending.shape[1]
    columns_rhs = pending.shape[2]
    if ascending:
        sequence = list(range(total_blocks))
    else:
        sequence = list(range(total_blocks - 1, -1, -1))
    solved = [None] * total_blocks
    for current in sequence:
        if ascending:
            later = slice(current + 1, total_blocks)
        else:
            later = slice(0, current)
        rounded = pending[current].astype(jnp.bfloat16)
        couple_rows = coupling[later]
        waiting = couple_rows.shape[0]
        own_inverse = inverse[current]
        offset = current * SEP
        gathered = whole_of(rounded, (("blk_0", "blk_1"), "blk_2"), 0)
        result = jnp.dot(own_inverse, gathered, preferred_element_type=jnp.float32)
        couple_cols = couple_rows[:, :, offset : offset + SEP].reshape(waiting * row_count, SEP)
        update = jnp.dot(couple_cols, gathered, preferred_element_type=jnp.float32)
        solved[current] = result
        if waiting > 0:
            pending = pending.at[later].add(-update.reshape(waiting, row_count, columns_rhs))
    return jnp.stack(solved)


def shards(lower_coupling, upper_coupling, lower_inverse, upper_inverse, right_side):
    intermediate = sweep(right_side, lower_coupling, lower_inverse, True)
    return sweep(intermediate, upper_coupling, upper_inverse, False)


def solution(mesh):
    finer = Mesh(
        mesh.devices.reshape(4, 4, 2, mesh.shape["rhs"]), ("blk_0", "blk_1", "blk_2", "rhs")
    )
    in_specs = (
        P(None, BLK, None),
        P(None, BLK, None),
        P(None, BLK, None),
        P(None, BLK, None),
        P(None, BLK, "rhs"),
    )
    out_specs = P(None, BLK, "rhs")
    return jax.shard_map(
        shards, mesh=finer, in_specs=in_specs, out_specs=out_specs, check_vma=False
    )
```

profile of v0, /device:TPU:1, one launch (start us, length us, event | category | flops | bytes accessed | tf_op | source)
XLA Modules:
  0.0 186.1 jit_solution(17539785398644807952)
XLA Ops:
  0.0 1.0 fusion.21
  1.0 0.3 broadcast_in_dim.21
  1.2 33.6 %all_to_all.40 = bf16[16,64,1024]{2,1,0:T(8,128)(2,1)S(1)} all-to-all(bf16[16,64,1024]{2,1,0:T(8,128)(2,1)S(1)} %broadcast_in_dim.21), channel_id=1, replica_groups=mesh['blk_0'=4,'blk_1'=4,'blk_2'=2,'rhs'=16] {'blk_0','blk_1'}, dimensions={0} | all-to-all | bytes 4194304 | tf_op jit(solution)/shard_map/all_to_all | solution.py:13
  34.8 0.6 broadcast_in_dim.22
  35.5 9.8 %all_to_all.41 = bf16[2,16,64,1024]{3,2,1,0:T(8,128)(2,1)S(1)} all-to-all(bf16[2,16,64,1024]{3,2,1,0:T(8,128)(2,1)S(1)} %broadcast_in_dim.22), channel_id=1, replica_groups=mesh['blk_0'=4,'blk_1'=4,'blk_2'=2,'rhs'=16] {'blk_2'}, dimensions={0} | all-to-all | bytes 8388608 | tf_op jit(solution)/shard_map/all_to_all | solution.py:13
  45.3 0.0 copy-start.4
  45.3 0.7 copy.6
  46.0 0.0 copy-start
  46.0 0.3 copy-done.4
  46.3 2.0 %fusion.7 = bf16[64,1024]{1,0:T(8,128)(2,1)S(1)} fusion(bf16[2048,1024]{1,0:T(8,128)(2,1)S(1)} %bitcast.64, bf16[2,64,4096]{2,1,0:T(8,128)(2,1)} %param.9, f32[2,64,1024]{2,1,0:T(8,128)S(1)} %copy-done.4), kind=kOutput, calls=%fused_computation.12 | convolution fusion | flops 268632064 | bytes 4849664 | tf_op jit(solution)/shard_map/dot_general | solution.py:53
  48.3 0.3 broadcast_in_dim.24
  48.6 30.2 %all_to_all.42 = bf16[16,64,1024]{2,1,0:T(8,128)(2,1)S(1)} all-to-all(bf16[16,64,1024]{2,1,0:T(8,128)(2,1)S(1)} %broadcast_in_dim.24), channel_id=1, replica_groups=mesh['blk_0'=4,'blk_1'=4,'blk_2'=2,'rhs'=16] {'blk_0','blk_1'}, dimensions={0} | all-to-all | bytes 4194304 | tf_op jit(solution)/shard_map/all_to_all | solution.py:13
  78.8 0.0 copy-done
  78.8 0.6 broadcast_in_dim.25
  79.4 8.8 %all_to_all.43 = bf16[2,16,64,1024]{3,2,1,0:T(8,128)(2,1)S(1)} all-to-all(bf16[2,16,64,1024]{3,2,1,0:T(8,128)(2,1)S(1)} %broadcast_in_dim.25), channel_id=1, replica_groups=mesh['blk_0'=4,'blk_1'=4,'blk_2'=2,'rhs'=16] {'blk_2'}, dimensions={0} | all-to-all | bytes 8388608 | tf_op jit(solution)/shard_map/all_to_all | solution.py:13
  88.2 0.0 copy-start.2
  88.2 0.7 copy.7
  88.9 0.3 copy-done.2
  89.3 0.9 fusion.6
  90.1 1.6 broadcast_in_dim.26
  91.7 3.7 %all-to-all-start.4 = ((bf16[16,64,1024]{2,1,0:T(8,128)(2,1)}), bf16[16,64,1024]{2,1,0:T(8,128)(2,1)S(1)}, u32[]{:S(2)}, u32[]{:S(2)}) async-start(bf16[16,64,1024]{2,1,0:T(8,128)(2,1)} %broadcast_in_dim.26), calls=%async_computation.4 | async-start | bytes 4194304 | tf_op jit(solution)/shard_map/all_to_all | solution.py:13
  95.4 3.0 %fusion.13 = f32[64,1024]{1,0:T(8,128)S(1)} fusion(bf16[2048,1024]{1,0:T(8,128)(2,1)} %bitcast.65, bf16[2,64,2048]{2,1,0:T(8,128)(2,1)S(1)} %copy-done.2), kind=kOutput, calls=%fused_computation.20 | convolution fusion | flops 268435456 | bytes 4718592 | tf_op jit(solution)/shard_map/dot_general | solution.py:51
  98.5 26.1 %all-to-all-done.4 = bf16[16,64,1024]{2,1,0:T(8,128)(2,1)S(1)} async-done(((bf16[16,64,1024]{2,1,0:T(8,128)(2,1)}), bf16[16,64,1024]{2,1,0:T(8,128)(2,1)S(1)}, u32[]{:S(2)}, u32[]{:S(2)}) %all-to-all-start.4) | async-done | bytes 2097184 | tf_op jit(solution)/shard_map/all_to_all | solution.py:13
  124.6 0.5 broadcast_in_dim.27
  125.1 8.7 %all_to_all.44 = bf16[2,16,64,1024]{3,2,1,0:T(8,128)(2,1)S(1)} all-to-all(bf16[2,16,64,1024]{3,2,1,0:T(8,128)(2,1)S(1)} %broadcast_in_dim.27), channel_id=1, replica_groups=mesh['blk_0'=4,'blk_1'=4,'blk_2'=2,'rhs'=16] {'blk_2'}, dimensions={0} | all-to-all | bytes 8388608 | tf_op jit(solution)/shard_map/all_to_all | solution.py:13
  133.8 0.7 copy.8
  134.5 0.0 copy-start.1
  134.5 1.9 %copy-done.1 = bf16[2,16,64,1024]{3,2,0,1:T(8,128)(2,1)} copy-done((bf16[2,16,64,1024]{3,2,0,1:T(8,128)(2,1)}, bf16[2,16,64,1024]{3,2,0,1:T(8,128)(2,1)S(1)}, u32[]{:S(2)}) %copy-start.1) | copy-done | bytes 4194328
  136.4 1.8 fusion.5
  138.2 0.0 copy-start.3
  138.2 1.6 broadcast_in_dim.28
  139.8 4.7 %all-to-all-start.6 = ((bf16[16,64,1024]{2,1,0:T(8,128)(2,1)}), bf16[16,64,1024]{2,1,0:T(8,128)(2,1)S(1)}, u32[]{:S(2)}, u32[]{:S(2)}) async-start(bf16[16,64,1024]{2,1,0:T(8,128)(2,1)} %broadcast_in_dim.28), calls=%async_computation.6 | async-start | bytes 4194304 | tf_op jit(solution)/shard_map/all_to_all | solution.py:13
  144.6 0.0 copy-done.3
  144.6 3.0 %convolution_bitcast_fusion = f32[1,64,1024]{2,1,0:T(8,128)S(1)} fusion(bf16[2048,1024]{1,0:T(8,128)(2,1)} %bitcast.67, bf16[2,64,2048]{2,1,0:T(8,128)(2,1)S(1)} %copy-done.3), kind=kOutput, calls=%fused_computation | convolution fusion | flops 268435456 | bytes 4718592 | tf_op jit(solution)/shard_map/dot_general | solution.py:51
  147.6 26.2 %all-to-all-done.6 = bf16[16,64,1024]{2,1,0:T(8,128)(2,1)S(1)} async-done(((bf16[16,64,1024]{2,1,0:T(8,128)(2,1)}), bf16[16,64,1024]{2,1,0:T(8,128)(2,1)S(1)}, u32[]{:S(2)}, u32[]{:S(2)}) %all-to-all-start.6) | async-done | bytes 2097184 | tf_op jit(solution)/shard_map/all_to_all | solution.py:13
  173.8 0.5 broadcast_in_dim.29
  174.4 9.3 %all_to_all.45 = bf16[2,16,64,1024]{3,2,1,0:T(8,128)(2,1)S(1)} all-to-all(bf16[2,16,64,1024]{3,2,1,0:T(8,128)(2,1)S(1)} %broadcast_in_dim.29), channel_id=1, replica_groups=mesh['blk_0'=4,'blk_1'=4,'blk_2'=2,'rhs'=16] {'blk_2'}, dimensions={0} | all-to-all | bytes 8388608 | tf_op jit(solution)/shard_map/all_to_all | solution.py:13
  183.7 0.7 copy.9
  184.4 0.9 convolution_bitcast_fusion.1
  185.2 0.8 pad_maximum_fusion
Async XLA Ops:
  45.3 1.0 copy-start.4
  46.0 32.8 %copy-start = (bf16[2,16,64,1024]{3,2,0,1:T(8,128)(2,1)}, bf16[2,16,64,1024]{3,2,0,1:T(8,128)(2,1)S(1)}, u32[]{:S(2)}) copy-start(bf16[2,16,64,1024]{3,2,0,1:T(8,128)(2,1)S(1)} %copy.6) | copy-start | bytes 12582916
  88.2 1.0 copy-start.2
  91.7 32.9 %all-to-all-start.4 = ((bf16[16,64,1024]{2,1,0:T(8,128)(2,1)}), bf16[16,64,1024]{2,1,0:T(8,128)(2,1)S(1)}, u32[]{:S(2)}, u32[]{:S(2)}) async-start(bf16[16,64,1024]{2,1,0:T(8,128)(2,1)} %broadcast_in_dim.26), calls=%async_computation.4 | async-start | bytes 4194304 | tf_op jit(solution)/shard_map/all_to_all | solution.py:13
  134.5 1.9 %copy-start.1 = (bf16[2,16,64,1024]{3,2,0,1:T(8,128)(2,1)}, bf16[2,16,64,1024]{3,2,0,1:T(8,128)(2,1)S(1)}, u32[]{:S(2)}) copy-start(bf16[2,16,64,1024]{3,2,0,1:T(8,128)(2,1)S(1)} %copy.8) | copy-start | bytes 12582916
  138.2 6.3 %copy-start.3 = (bf16[2,64,2048]{2,1,0:T(8,128)(2,1)S(1)}, bf16[2,64,2048]{2,1,0:T(8,128)(2,1)}, u32[]{:S(2)}) copy-start(bf16[2,64,2048]{2,1,0:T(8,128)(2,1)} %param.12) | copy-start | bytes 1572868
  139.8 34.0 %all-to-all-start.6 = ((bf16[16,64,1024]{2,1,0:T(8,128)(2,1)}), bf16[16,64,1024]{2,1,0:T(8,128)(2,1)S(1)}, u32[]{:S(2)}, u32[]{:S(2)}) async-start(bf16[16,64,1024]{2,1,0:T(8,128)(2,1)} %broadcast_in_dim.28), calls=%async_computation.6 | async-start | bytes 4194304 | tf_op jit(solution)/shard_map/all_to_all | solution.py:13
where the time goes:
time: 187 us; the launch traced here: 186 us
  blocking collectives  100 us (53%)
  waiting for transfers between devices  52.3 us (28%)
  local copies, waits for them, and re-layouts  12.3 us (7%)
  matrix products  11.6 us (6%)
  starting transfers between devices  8.46 us (5%)
    all_to_all x6, blocking collectives, from_everyone(): lax.all_to_all(jnp.broadcast_to(array[None], (size, *array.shape)), axis,...  100 us
    all_to_all x2, waiting for transfers between devices, from_everyone(): lax.all_to_all(jnp.broadcast_to(array[None], (size, *array.shape)), axis,...  52.3 us
    all_to_all x2, starting transfers between devices, from_everyone(): lax.all_to_all(jnp.broadcast_to(array[None], (size, *array.shape)), axis,...  8.46 us
    dot_general x4, matrix products, sweep(): result = jnp.dot(own_inverse, gathered, preferred_element_type=jnp.float32)  7.76 us
    broadcast_in_dim x9, local copies, waits for them, and re-layouts, from_everyone(): jnp.broadcast_to(array[None], (size, *array.shape))  6.93 us
    dot_general x2, matrix products, sweep(): update = jnp.dot(couple_cols, gathered, preferred_element_type=jnp.float32)  3.82 us
  transfers between devices with their start and end apart: 2, of which 2 were waited for; matrix products, arithmetic and copies ran while one was open for 3% of the time, Pallas kernels for 0%

commit v1 on v0

v1 whole, which is shorter than its diff:
```python
import functools

import jax
import jax.numpy as jnp
from jax import lax
from jax.experimental import pallas as pl
from jax.experimental.pallas import tpu as pltpu
from jax.sharding import Mesh
from jax.sharding import PartitionSpec as P

BLK = ("blk_0", "blk_1", "blk_2")
L10, LI1, U01, LI0, UI1, UI0 = range(6)


def kernel(
    depth_z, lc, li, uc, ui, b, o,
    w, v, bv, fst, b1g, acc, y0, ob, ro,
    hsem, ysend, yrecv, msend, mrecv, asend, arecv, bsend, brecv, xsend, xrecv,
):
    rows, cols = fst.shape[1], fst.shape[2]
    own = 4 * rows
    span = 2 * rows
    x, y, k, z = (lax.axis_index(a) for a in BLK + ("rhs",))
    xr, xl, xo = (x + 1) % 4, (x + 3) % 4, (x + 2) % 4
    yr, yl, yo = (y + 1) % 4, (y + 3) % 4, (y + 2) % 4
    zr, zl = (z + 1) % depth_z, (z + depth_z - 1) % depth_z
    p = z % 2
    q = 1 - p
    sib = 1 - k
    RIGHT, LEFT = (xr, y, k, z), (xl, y, k, z)
    UP, DOWN = (x, yr, k, z), (x, yl, k, z)
    NEXT, BACK = (x, y, k, zr), (x, y, k, zl)
    SIB = (x, y, sib, z)

    def remote(src, dst, ssem, rsem, dev):
        return pltpu.make_async_remote_copy(
            src_ref=src, dst_ref=dst, send_sem=ssem, recv_sem=rsem,
            device_id=dev, device_id_type=pl.DeviceIdType.MESH,
        )

    sent = []

    def send(src, sends, recvs, i, dev, dst=None):
        c = remote(src, src if dst is None else dst, sends.at[i], recvs.at[i], dev)
        c.start()
        sent.append(c)

    def arrived(ref, sends, recvs, i, dev):
        remote(ref, ref, sends.at[i], recvs.at[i], dev).wait_recv()

    barrier = pltpu.get_barrier_semaphore()
    greeted = [RIGHT, LEFT, (xo, y, k, z), UP, DOWN, SIB, NEXT, BACK]
    for dev in greeted:
        pl.semaphore_signal(barrier, inc=1, device_id=dev, device_id_type=pl.DeviceIdType.MESH)

    loads_b = [
        [
            pltpu.make_async_copy(b.at[s, :, c * cols:(c + 1) * cols], bv.at[s, c], hsem.at[s, c])
            for c in range(4)
        ]
        for s in range(2)
    ]
    sep = 32 * rows
    source = [
        lc.at[1, :, :, :, 0:sep], li.at[1], uc.at[0, :, :, :, sep:2 * sep],
        li.at[0], ui.at[1], ui.at[0],
    ]
    loads_w = [pltpu.make_async_copy(source[m], w.at[m, x], hsem.at[2 + m // 4, m % 4]) for m in range(6)]
    for c in loads_b[0]:
        c.start()
    loads_w[0].start()
    for c in loads_b[1]:
        c.start()
    for c in loads_w[1:]:
        c.start()
    for c in range(4):
        loads_b[0][c].wait()
        fst[c] = bv[0, c].astype(jnp.bfloat16)
    v[0, x, y, k] = fst[x]

    pl.semaphore_wait(barrier, len(greeted))

    def own_send(m):
        loads_w[m].wait()
        send(w.at[m, x, p], msend.at[m], mrecv.at[m], 0, RIGHT)
        send(w.at[m, x, p], msend.at[m], mrecv.at[m], 1, LEFT)

    def relay(m):
        s, r = msend.at[m], mrecv.at[m]
        arrived(w.at[m, xl, p], s, r, 0, LEFT)
        send(w.at[m, xl, p, 0], s, r, 2, RIGHT)
        send(w.at[m, xl, p, 0], s, r, 4, NEXT)
        send(w.at[m, xl, p, 1], s, r, 5, BACK)
        arrived(w.at[m, xr, p], s, r, 1, RIGHT)
        send(w.at[m, xr, p, 1], s, r, 3, LEFT)
        send(w.at[m, xr, p, 0], s, r, 6, NEXT)
        send(w.at[m, xr, p, 1], s, r, 7, BACK)

    def relay_far(m):
        s, r = msend.at[m], mrecv.at[m]
        arrived(w.at[m, xo, p, 0], s, r, 2, LEFT)
        send(w.at[m, xo, p, 0], s, r, 8, NEXT)
        arrived(w.at[m, xo, p, 1], s, r, 3, RIGHT)
        send(w.at[m, xo, p, 1], s, r, 9, BACK)

    def complete(m):
        s, r = msend.at[m], mrecv.at[m]
        for i, (src, part) in enumerate([(xl, 0), (xl, 1), (xr, 0), (xr, 1), (xo, 0), (xo, 1)]):
            arrived(w.at[m, src, q, part], s, r, 4 + i, BACK if part == 0 else NEXT)

    def product(m, s, yy):
        lhs = jnp.concatenate(
            [
                w[m, :, :, :, :, pl.ds(pl.multiple_of(c * 4 * span + yy * span, span), span)].reshape(own, span)
                for c in range(4)
            ],
            axis=1,
        )
        rhs = v[s, :, yy].reshape(4 * span, cols)
        return jnp.dot(lhs, rhs, preferred_element_type=jnp.float32)

    def full_product(m, s, dst):
        dst[...] = product(m, s, 0)
        for yy in range(1, 4):
            dst[...] += product(m, s, yy)

    def gather(s, m, early=None, middle=None, late=None):
        ss, rr = ysend.at[s], yrecv.at[s]
        mine = v.at[s, :, y, k]
        send(v.at[s, 0:2, y, k], ss, rr, 0, UP)
        send(v.at[s, 2:4, y, k], ss, rr, 2, DOWN)
        send(v.at[s, 2:4, y, k], ss, rr, 1, UP)
        send(v.at[s, 0:2, y, k], ss, rr, 3, DOWN)
        send(mine, ss, rr, 6, SIB)
        if early is not None:
            early()
        arrived(v.at[s, 0:2, yl, k], ss, rr, 0, DOWN)
        send(v.at[s, 0:2, yl, k], ss, rr, 4, UP)
        send(v.at[s, 0:2, yl, k], ss, rr, 7, SIB)
        arrived(v.at[s, 2:4, yr, k], ss, rr, 2, UP)
        send(v.at[s, 2:4, yr, k], ss, rr, 5, DOWN)
        send(v.at[s, 2:4, yr, k], ss, rr, 9, SIB)
        if middle is not None:
            middle()
        arrived(v.at[s, :, y, sib], ss, rr, 6, SIB)
        acc[...] = product(m, s, y)
        arrived(v.at[s, 2:4, yl, k], ss, rr, 1, DOWN)
        send(v.at[s, 2:4, yl, k], ss, rr, 8, SIB)
        arrived(v.at[s, 0:2, yr, k], ss, rr, 3, UP)
        send(v.at[s, 0:2, yr, k], ss, rr, 10, SIB)
        if late is not None:
            late()
        arrived(v.at[s, 0:2, yl, sib], ss, rr, 7, SIB)
        arrived(v.at[s, 2:4, yl, sib], ss, rr, 8, SIB)
        acc[...] += product(m, s, yl)
        arrived(v.at[s, 0:2, yo, k], ss, rr, 4, DOWN)
        send(v.at[s, 0:2, yo, k], ss, rr, 11, SIB)
        arrived(v.at[s, 2:4, yo, k], ss, rr, 5, UP)
        send(v.at[s, 2:4, yo, k], ss, rr, 12, SIB)
        arrived(v.at[s, 2:4, yr, sib], ss, rr, 9, SIB)
        arrived(v.at[s, 0:2, yr, sib], ss, rr, 10, SIB)
        acc[...] += product(m, s, yr)
        arrived(v.at[s, 0:2, yo, sib], ss, rr, 11, SIB)
        arrived(v.at[s, 2:4, yo, sib], ss, rr, 12, SIB)
        acc[...] += product(m, s, yo)

    def result(s):
        ob[s] = acc[...].reshape(4, rows, cols).astype(jnp.bfloat16)
        for d in (2, 1, 3):
            send(ob.at[s, (x + d) % 4], xsend.at[s], xrecv.at[s], d, ((x + d) % 4, y, k, z), ro.at[s, x])

    def write(s):
        ro[s, x] = ob[s, x]
        for d in (1, 3, 2):
            arrived(ro.at[s, (x + 4 - d) % 4], xsend.at[s], xrecv.at[s], d, ((x + 4 - d) % 4, y, k, z))
        for c in range(4):
            o[s, :, c * cols:(c + 1) * cols] = ro[s, c].astype(jnp.float32)

    for d in (2, 1, 3):
        send(fst.at[(x + d) % 4], asend, arecv, d, ((x + d) % 4, y, k, z), v.at[0, x, y, k])
    own_send(L10)
    for d in (1, 3, 2):
        arrived(v.at[0, (x + 4 - d) % 4, y, k], asend, arecv, d, ((x + 4 - d) % 4, y, k, z))

    def middle_0():
        relay(L10)
        own_send(LI1)
        for c in loads_b[1]:
            c.wait()
        b1g[x] = bv[1, x]
        for d in (2, 1, 3):
            send(bv.at[1, (x + d) % 4], bsend, brecv, d, ((x + d) % 4, y, k, z), b1g.at[x])

    def late_0():
        relay_far(L10)
        relay(LI1)
        own_send(U01)
        complete(L10)

    def gather_first():
        s = 0
        ss, rr = ysend.at[s], yrecv.at[s]
        send(v.at[s, 0:2, y, k], ss, rr, 0, UP)
        send(v.at[s, 2:4, y, k], ss, rr, 2, DOWN)
        send(v.at[s, 2:4, y, k], ss, rr, 1, UP)
        send(v.at[s, 0:2, y, k], ss, rr, 3, DOWN)
        send(v.at[s, :, y, k], ss, rr, 6, SIB)
        arrived(v.at[s, 0:2, yl, k], ss, rr, 0, DOWN)
        send(v.at[s, 0:2, yl, k], ss, rr, 4, UP)
        send(v.at[s, 0:2, yl, k], ss, rr, 7, SIB)
        arrived(v.at[s, 2:4, yr, k], ss, rr, 2, UP)
        send(v.at[s, 2:4, yr, k], ss, rr, 5, DOWN)
        send(v.at[s, 2:4, yr, k], ss, rr, 9, SIB)
        middle_0()
        arrived(v.at[s, 2:4, yl, k], ss, rr, 1, DOWN)
        send(v.at[s, 2:4, yl, k], ss, rr, 8, SIB)
        arrived(v.at[s, 0:2, yr, k], ss, rr, 3, UP)
        send(v.at[s, 0:2, yr, k], ss, rr, 10, SIB)
        arrived(v.at[s, 0:2, yo, k], ss, rr, 4, DOWN)
        send(v.at[s, 0:2, yo, k], ss, rr, 11, SIB)
        arrived(v.at[s, 2:4, yo, k], ss, rr, 5, UP)
        send(v.at[s, 2:4, yo, k], ss, rr, 12, SIB)
        late_0()
        arrived(v.at[s, :, y, sib], ss, rr, 6, SIB)
        arrived(v.at[s, 0:2, yl, sib], ss, rr, 7, SIB)
        arrived(v.at[s, 2:4, yl, sib], ss, rr, 8, SIB)
        arrived(v.at[s, 2:4, yr, sib], ss, rr, 9, SIB)
        arrived(v.at[s, 0:2, yr, sib], ss, rr, 10, SIB)
        arrived(v.at[s, 0:2, yo, sib], ss, rr, 11, SIB)
        arrived(v.at[s, 2:4, yo, sib], ss, rr, 12, SIB)
        full_product(L10, 0, acc)

    gather_first()
    for d in (1, 3, 2):
        arrived(b1g.at[(x + 4 - d) % 4], bsend, brecv, d, ((x + 4 - d) % 4, y, k, z))

    def residual(s, values):
        v[s, :, y, k] = values.astype(jnp.bfloat16).reshape(4, rows, cols)

    residual(1, b1g[...].reshape(own, cols) - acc[...])

    def middle_1():
        relay_far(LI1)
        relay(U01)
        own_send(LI0)
        complete(LI1)

    gather(1, LI1, middle=middle_1, late=lambda: relay_far(U01))

    residual(2, acc[...])

    def early_2():
        relay(LI0)
        own_send(UI1)
        complete(U01)

    def middle_2():
        relay_far(LI0)
        relay(UI1)
        own_send(UI0)

    def late_2():
        complete(LI0)
        full_product(LI0, 0, y0)
        relay_far(UI1)

    gather(2, U01, early=early_2, middle=middle_2, late=late_2)

    residual(3, y0[...] - acc[...])

    def early_3():
        relay(UI0)

    def middle_3():
        complete(UI1)
        full_product(UI1, 2, acc)
        result(1)
        relay_far(UI0)
        complete(UI0)

    gather(3, UI0, early=early_3, middle=middle_3)
    result(0)
    write(1)
    write(0)
    for c in sent:
        c.wait_send()


def shards(depth_z, lower_coupling, upper_coupling, lower_inverse, upper_inverse, right_side):
    rows = right_side.shape[1]
    cols = right_side.shape[2] // 4
    quarter = rows // 4

    def split(a):
        return a.reshape(2, 2, 2, quarter, a.shape[2])

    f32, bf16 = jnp.float32, jnp.bfloat16
    dma = pltpu.SemaphoreType.DMA
    hbm = pl.BlockSpec(memory_space=pltpu.MemorySpace.HBM)
    return pl.pallas_call(
        functools.partial(kernel, depth_z),
        out_shape=jax.ShapeDtypeStruct(right_side.shape, f32),
        in_specs=[hbm] * 5,
        out_specs=pl.BlockSpec(memory_space=pltpu.MemorySpace.VMEM),
        scratch_shapes=[
            pltpu.VMEM((6, 4, 2, 2, quarter, 32 * rows), bf16),
            pltpu.VMEM((4, 4, 4, 2, rows, cols), bf16),
            pltpu.VMEM((2, 4, rows, cols), f32),
            pltpu.VMEM((4, rows, cols), bf16),
            pltpu.VMEM((4, rows, cols), f32),
            pltpu.VMEM((4 * rows, cols), f32),
            pltpu.VMEM((4 * rows, cols), f32),
            pltpu.VMEM((2, 4, rows, cols), bf16),
            pltpu.VMEM((2, 4, rows, cols), bf16),
            dma((4, 4)),
            dma((4, 13)), dma((4, 13)),
            dma((6, 10)), dma((6, 10)),
            dma((4,)), dma((4,)),
            dma((4,)), dma((4,)),
            dma((2, 4)), dma((2, 4)),
        ],
        compiler_params=pltpu.CompilerParams(
            collective_id=0, has_side_effects=True, vmem_limit_bytes=48 * 2**20
        ),
    )(split(lower_coupling), split(lower_inverse), split(upper_coupling), split(upper_inverse), right_side)


def solution(mesh):
    depth_z = mesh.shape["rhs"]
    finer = Mesh(mesh.devices.reshape(4, 4, 2, depth_z), BLK + ("rhs",))
    spec = P(None, BLK, None)
    return jax.shard_map(
        functools.partial(shards, depth_z),
        mesh=finer,
        in_specs=(spec, spec, spec, spec, P(None, BLK, "rhs")),
        out_specs=P(None, BLK, "rhs"),
        check_vma=False,
    )
```

time: 187 us -> 78 us (0.42)
  blocking collectives: 100 us -> 0 us
  Pallas kernels: 0 us -> 71.3 us
  waiting for transfers between devices: 52.3 us -> 0 us
  matrix products: 11.6 us -> 0 us
  starting transfers between devices: 8.46 us -> 0 us
  local copies, waits for them, and re-layouts: 12.3 us -> 6.37 us
    all_to_all x6 -> x0, blocking collectives: 100 us -> none  [from_everyone(): lax.all_to_all(jnp.broadcast_to(array[None], (size, *array.shape)), axis,...]
    pallas_call x0 -> x1, Pallas kernels: none -> 71.3 us  [shards(): pl.pallas_call(functools.partial(kernel, depth_z), out_shape=jax.ShapeDty...]
    all_to_all x2 -> x0, waiting for transfers between devices: 52.3 us -> none  [from_everyone(): lax.all_to_all(jnp.broadcast_to(array[None], (size, *array.shape)), axis,...]
    dot_general x6 -> x0, matrix products: 11.6 us -> none  [the longest x4 7.76 us: sweep(): result = jnp.dot(own_inverse, gathered, preferred_element_type=jnp.float32)]
    all_to_all x2 -> x0, starting transfers between devices: 8.46 us -> none  [from_everyone(): lax.all_to_all(jnp.broadcast_to(array[None], (size, *array.shape)), axis,...]
    broadcast_in_dim x9 -> x0, local copies, waits for them, and re-layouts: 6.93 us -> none  [from_everyone(): jnp.broadcast_to(array[None], (size, *array.shape))]
    unnamed x10 -> x11, local copies, waits for them, and re-layouts: 2.59 us -> 6.37 us
    all_to_all x4 -> x0, local copies, waits for them, and re-layouts: 2.81 us -> none  [from_everyone(): lax.all_to_all(jnp.broadcast_to(array[None], (size, *array.shape)), axis,...]
  transfers between devices with their start and end apart: 2 -> 0, of which waited for: 2 -> 0; matrix products, arithmetic and copies ran while one was open for 3% -> 0% of each run, Pallas kernels for 0% -> 0%
where the time goes in v1:
time: 78 us; the launch traced here: 77.7 us
  Pallas kernels  71.3 us (91%)
  local copies, waits for them, and re-layouts  6.37 us (8%)
    pallas_call x1, Pallas kernels, shards(): pl.pallas_call(functools.partial(kernel, depth_z), out_shape=jax.ShapeDty...  71.3 us
    unnamed x11, local copies, waits for them, and re-layouts  6.37 us

profile of v1, /device:TPU:1, one launch (start us, length us, event | category | flops | bytes accessed | tf_op | source)
XLA Modules:
  0.0 77.7 jit_solution(1646217960778342734)
XLA Ops:
  0.0 0.0 copy-start
  0.0 1.2 %copy-done = bf16[2,64,4096]{2,1,0:T(8,128)(2,1)S(1)} copy-done((bf16[2,64,4096]{2,1,0:T(8,128)(2,1)S(1)}, bf16[2,64,4096]{2,1,0:T(8,128)(2,1)}, u32[]{:S(2)}) %copy-start) | copy-done | bytes 1048600
  1.2 0.0 copy-start.1
  1.2 1.2 %copy-done.1 = bf16[2,64,4096]{2,1,0:T(8,128)(2,1)S(1)} copy-done((bf16[2,64,4096]{2,1,0:T(8,128)(2,1)S(1)}, bf16[2,64,4096]{2,1,0:T(8,128)(2,1)}, u32[]{:S(2)}) %copy-start.1) | copy-done | bytes 1048600
  2.5 0.0 copy-start.2
  2.5 1.0 %copy-done.2 = bf16[2,64,2048]{2,1,0:T(8,128)(2,1)S(1)} copy-done((bf16[2,64,2048]{2,1,0:T(8,128)(2,1)S(1)}, bf16[2,64,2048]{2,1,0:T(8,128)(2,1)}, u32[]{:S(2)}) %copy-start.2) | copy-done | bytes 524312
  3.5 0.0 copy-start.3
  3.5 1.0 %copy-done.3 = bf16[2,64,2048]{2,1,0:T(8,128)(2,1)S(1)} copy-done((bf16[2,64,2048]{2,1,0:T(8,128)(2,1)S(1)}, bf16[2,64,2048]{2,1,0:T(8,128)(2,1)}, u32[]{:S(2)}) %copy-start.3) | copy-done | bytes 524312
  4.5 0.0 copy-start.4
  4.5 1.0 %copy-done.4 = f32[2,64,1024]{2,1,0:T(8,128)S(1)} copy-done((f32[2,64,1024]{2,1,0:T(8,128)S(1)}, f32[2,64,1024]{2,1,0:T(8,128)}, u32[]{:S(2)}) %copy-start.4) | copy-done | bytes 524312
  5.6 71.3 %shard_map.55 = f32[2,64,1024]{2,1,0:T(8,128)S(1)} custom-call(bf16[2,2,2,16,4096]{4,3,2,1,0:T(8,128)(2,1)S(1)} %bitcast.4, bf16[2,2,2,16,2048]{4,3,2,1,0:T(8,128)(2,1)S(1)} %bitcast.6, bf16[2,2,2,16,4096]{4,3,2,1,0:T(8,128)(2,1)S(1)} %bitcast.5, bf16[2,2,2,16,2048]{4,3,2,1,0:T(8,128)(2,1)S(1)} %bitcast.7, f32[2,64,1024]{2,1,0:T(8,128)S(1)} %copy-done.4), custom_call_target="tpu_custom_call" | custom-call | tf_op jit(solution)/shard_map/pallas_call | solution.py:300
  76.9 0.8 %copy.7 = f32[2,64,1024]{2,1,0:T(8,128)} copy(f32[2,64,1024]{2,1,0:T(8,128)S(1)} %shard_map.55) | data formatting | bytes 1048576
Async XLA Ops:
  0.0 1.2 %copy-start = (bf16[2,64,4096]{2,1,0:T(8,128)(2,1)S(1)}, bf16[2,64,4096]{2,1,0:T(8,128)(2,1)}, u32[]{:S(2)}) copy-start(bf16[2,64,4096]{2,1,0:T(8,128)(2,1)} %param.5) | copy-start | bytes 3145732
  1.2 1.2 %copy-start.1 = (bf16[2,64,4096]{2,1,0:T(8,128)(2,1)S(1)}, bf16[2,64,4096]{2,1,0:T(8,128)(2,1)}, u32[]{:S(2)}) copy-start(bf16[2,64,4096]{2,1,0:T(8,128)(2,1)} %param.6) | copy-start | bytes 3145732
  2.5 1.0 %copy-start.2 = (bf16[2,64,2048]{2,1,0:T(8,128)(2,1)S(1)}, bf16[2,64,2048]{2,1,0:T(8,128)(2,1)}, u32[]{:S(2)}) copy-start(bf16[2,64,2048]{2,1,0:T(8,128)(2,1)} %param.7) | copy-start | bytes 1572868
  3.5 1.0 %copy-start.3 = (bf16[2,64,2048]{2,1,0:T(8,128)(2,1)S(1)}, bf16[2,64,2048]{2,1,0:T(8,128)(2,1)}, u32[]{:S(2)}) copy-start(bf16[2,64,2048]{2,1,0:T(8,128)(2,1)} %param.8) | copy-start | bytes 1572868
  4.5 1.0 %copy-start.4 = (f32[2,64,1024]{2,1,0:T(8,128)S(1)}, f32[2,64,1024]{2,1,0:T(8,128)}, u32[]{:S(2)}) copy-start(f32[2,64,1024]{2,1,0:T(8,128)} %b.1) | copy-start | bytes 1572868

commit v2 on v1

--- a/solution.py
+++ b/solution.py
@@ -10,6 +10,8 @@
 
 BLK = ("blk_0", "blk_1", "blk_2")
 L10, LI1, U01, LI0, UI1, UI0 = range(6)
+DIRECT = (True,) * 6
+EARLY = (LI1, U01, LI0, UI1, UI0)
 
 
 def kernel(
@@ -31,6 +33,7 @@
     UP, DOWN = (x, yr, k, z), (x, yl, k, z)
     NEXT, BACK = (x, y, k, zr), (x, y, k, zl)
     SIB = (x, y, sib, z)
+    FAR = (xo, y, k, z)
 
     def remote(src, dst, ssem, rsem, dev):
         return pltpu.make_async_remote_copy(
@@ -49,7 +52,7 @@
         remote(ref, ref, sends.at[i], recvs.at[i], dev).wait_recv()
 
     barrier = pltpu.get_barrier_semaphore()
-    greeted = [RIGHT, LEFT, (xo, y, k, z), UP, DOWN, SIB, NEXT, BACK]
+    greeted = [RIGHT, LEFT, FAR, UP, DOWN, SIB, NEXT, BACK]
     for dev in greeted:
         pl.semaphore_signal(barrier, inc=1, device_id=dev, device_id_type=pl.DeviceIdType.MESH)
 
@@ -82,25 +85,38 @@
 
     def own_send(m):
         loads_w[m].wait()
-        send(w.at[m, x, p], msend.at[m], mrecv.at[m], 0, RIGHT)
-        send(w.at[m, x, p], msend.at[m], mrecv.at[m], 1, LEFT)
+        s, r = msend.at[m], mrecv.at[m]
+        send(w.at[m, x, p], s, r, 0, RIGHT)
+        send(w.at[m, x, p], s, r, 1, LEFT)
+        if DIRECT[m]:
+            send(w.at[m, x, p], s, r, 2, FAR)
+
+    def own_later(m):
+        if m not in EARLY:
+            own_send(m)
 
     def relay(m):
         s, r = msend.at[m], mrecv.at[m]
         arrived(w.at[m, xl, p], s, r, 0, LEFT)
-        send(w.at[m, xl, p, 0], s, r, 2, RIGHT)
+        if not DIRECT[m]:
+            send(w.at[m, xl, p, 0], s, r, 2, RIGHT)
         send(w.at[m, xl, p, 0], s, r, 4, NEXT)
         send(w.at[m, xl, p, 1], s, r, 5, BACK)
         arrived(w.at[m, xr, p], s, r, 1, RIGHT)
-        send(w.at[m, xr, p, 1], s, r, 3, LEFT)
+        if not DIRECT[m]:
+            send(w.at[m, xr, p, 1], s, r, 3, LEFT)
         send(w.at[m, xr, p, 0], s, r, 6, NEXT)
         send(w.at[m, xr, p, 1], s, r, 7, BACK)
 
     def relay_far(m):
         s, r = msend.at[m], mrecv.at[m]
-        arrived(w.at[m, xo, p, 0], s, r, 2, LEFT)
+        if DIRECT[m]:
+            arrived(w.at[m, xo, p], s, r, 2, FAR)
+        else:
+            arrived(w.at[m, xo, p, 0], s, r, 2, LEFT)
         send(w.at[m, xo, p, 0], s, r, 8, NEXT)
-        arrived(w.at[m, xo, p, 1], s, r, 3, RIGHT)
+        if not DIRECT[m]:
+            arrived(w.at[m, xo, p, 1], s, r, 3, RIGHT)
         send(w.at[m, xo, p, 1], s, r, 9, BACK)
 
     def complete(m):
@@ -124,48 +140,61 @@
         for yy in range(1, 4):
             dst[...] += product(m, s, yy)
 
-    def gather(s, m, early=None, middle=None, late=None):
+    def gather(s, m, start=None, near=None, second=None, far=None, ready=None):
         ss, rr = ysend.at[s], yrecv.at[s]
-        mine = v.at[s, :, y, k]
         send(v.at[s, 0:2, y, k], ss, rr, 0, UP)
         send(v.at[s, 2:4, y, k], ss, rr, 2, DOWN)
         send(v.at[s, 2:4, y, k], ss, rr, 1, UP)
         send(v.at[s, 0:2, y, k], ss, rr, 3, DOWN)
-        send(mine, ss, rr, 6, SIB)
-        if early is not None:
-            early()
+        send(v.at[s, :, y, k], ss, rr, 6, SIB)
+        if start is not None:
+            start()
         arrived(v.at[s, 0:2, yl, k], ss, rr, 0, DOWN)
         send(v.at[s, 0:2, yl, k], ss, rr, 4, UP)
         send(v.at[s, 0:2, yl, k], ss, rr, 7, SIB)
         arrived(v.at[s, 2:4, yr, k], ss, rr, 2, UP)
         send(v.at[s, 2:4, yr, k], ss, rr, 5, DOWN)
         send(v.at[s, 2:4, yr, k], ss, rr, 9, SIB)
-        if middle is not None:
-            middle()
-        arrived(v.at[s, :, y, sib], ss, rr, 6, SIB)
-        acc[...] = product(m, s, y)
+        if near is not None:
+            near()
         arrived(v.at[s, 2:4, yl, k], ss, rr, 1, DOWN)
         send(v.at[s, 2:4, yl, k], ss, rr, 8, SIB)
         arrived(v.at[s, 0:2, yr, k], ss, rr, 3, UP)
         send(v.at[s, 0:2, yr, k], ss, rr, 10, SIB)
-        if late is not None:
-            late()
-        arrived(v.at[s, 0:2, yl, sib], ss, rr, 7, SIB)
-        arrived(v.at[s, 2:4, yl, sib], ss, rr, 8, SIB)
-        acc[...] += product(m, s, yl)
+        if second is not None:
+            second()
+
+        def first_product():
+            arrived(v.at[s, :, y, sib], ss, rr, 6, SIB)
+            acc[...] = product(m, s, y)
+
+        def near_products():
+            arrived(v.at[s, 0:2, yl, sib], ss, rr, 7, SIB)
+            arrived(v.at[s, 2:4, yl, sib], ss, rr, 8, SIB)
+            acc[...] += product(m, s, yl)
+            arrived(v.at[s, 2:4, yr, sib], ss, rr, 9, SIB)
+            arrived(v.at[s, 0:2, yr, sib], ss, rr, 10, SIB)
+            acc[...] += product(m, s, yr)
+
+        if ready is None:
+            first_product()
+            near_products()
         arrived(v.at[s, 0:2, yo, k], ss, rr, 4, DOWN)
         send(v.at[s, 0:2, yo, k], ss, rr, 11, SIB)
         arrived(v.at[s, 2:4, yo, k], ss, rr, 5, UP)
         send(v.at[s, 2:4, yo, k], ss, rr, 12, SIB)
-        arrived(v.at[s, 2:4, yr, sib], ss, rr, 9, SIB)
-        arrived(v.at[s, 0:2, yr, sib], ss, rr, 10, SIB)
-        acc[...] += product(m, s, yr)
+        if far is not None:
+            far()
+        if ready is not None:
+            ready()
+            first_product()
+            near_products()
         arrived(v.at[s, 0:2, yo, sib], ss, rr, 11, SIB)
         arrived(v.at[s, 2:4, yo, sib], ss, rr, 12, SIB)
         acc[...] += product(m, s, yo)
 
-    def result(s):
-        ob[s] = acc[...].reshape(4, rows, cols).astype(jnp.bfloat16)
+    def result(s, total):
+        ob[s] = total[...].reshape(4, rows, cols).astype(jnp.bfloat16)
         for d in (2, 1, 3):
             send(ob.at[s, (x + d) % 4], xsend.at[s], xrecv.at[s], d, ((x + d) % 4, y, k, z), ro.at[s, x])
 
@@ -176,110 +205,73 @@
         for c in range(4):
             o[s, :, c * cols:(c + 1) * cols] = ro[s, c].astype(jnp.float32)
 
-    for d in (2, 1, 3):
+    def residual(s, values):
+        v[s, :, y, k] = values.astype(jnp.bfloat16).reshape(4, rows, cols)
+
+    def in_turn(*steps):
+        def run():
+            for step in steps:
+                step()
+        return run
+
+    def do(step, *args):
+        return functools.partial(step, *args)
+
+    for d in (1, 3, 2):
         send(fst.at[(x + d) % 4], asend, arecv, d, ((x + d) % 4, y, k, z), v.at[0, x, y, k])
     own_send(L10)
+    for c in loads_b[1]:
+        c.wait()
+    b1g[x] = bv[1, x]
+    for d in (1, 3, 2):
+        send(bv.at[1, (x + d) % 4], bsend, brecv, d, ((x + d) % 4, y, k, z), b1g.at[x])
+    for m in EARLY:
+        own_send(m)
     for d in (1, 3, 2):
         arrived(v.at[0, (x + 4 - d) % 4, y, k], asend, arecv, d, ((x + 4 - d) % 4, y, k, z))
-
-    def middle_0():
-        relay(L10)
-        own_send(LI1)
-        for c in loads_b[1]:
-            c.wait()
-        b1g[x] = bv[1, x]
-        for d in (2, 1, 3):
-            send(bv.at[1, (x + d) % 4], bsend, brecv, d, ((x + d) % 4, y, k, z), b1g.at[x])
-
-    def late_0():
-        relay_far(L10)
-        relay(LI1)
-        own_send(U01)
-        complete(L10)
-
-    def gather_first():
-        s = 0
-        ss, rr = ysend.at[s], yrecv.at[s]
-        send(v.at[s, 0:2, y, k], ss, rr, 0, UP)
-        send(v.at[s, 2:4, y, k], ss, rr, 2, DOWN)
-        send(v.at[s, 2:4, y, k], ss, rr, 1, UP)
-        send(v.at[s, 0:2, y, k], ss, rr, 3, DOWN)
-        send(v.at[s, :, y, k], ss, rr, 6, SIB)
-        arrived(v.at[s, 0:2, yl, k], ss, rr, 0, DOWN)
-        send(v.at[s, 0:2, yl, k], ss, rr, 4, UP)
-        send(v.at[s, 0:2, yl, k], ss, rr, 7, SIB)
-        arrived(v.at[s, 2:4, yr, k], ss, rr, 2, UP)
-        send(v.at[s, 2:4, yr, k], ss, rr, 5, DOWN)
-        send(v.at[s, 2:4, yr, k], ss, rr, 9, SIB)
-        middle_0()
-        arrived(v.at[s, 2:4, yl, k], ss, rr, 1, DOWN)
-        send(v.at[s, 2:4, yl, k], ss, rr, 8, SIB)
-        arrived(v.at[s, 0:2, yr, k], ss, rr, 3, UP)
-        send(v.at[s, 0:2, yr, k], ss, rr, 10, SIB)
-        arrived(v.at[s, 0:2, yo, k], ss, rr, 4, DOWN)
-        send(v.at[s, 0:2, yo, k], ss, rr, 11, SIB)
-        arrived(v.at[s, 2:4, yo, k], ss, rr, 5, UP)
-        send(v.at[s, 2:4, yo, k], ss, rr, 12, SIB)
-        late_0()
-        arrived(v.at[s, :, y, sib], ss, rr, 6, SIB)
-        arrived(v.at[s, 0:2, yl, sib], ss, rr, 7, SIB)
-        arrived(v.at[s, 2:4, yl, sib], ss, rr, 8, SIB)
-        arrived(v.at[s, 2:4, yr, sib], ss, rr, 9, SIB)
-        arrived(v.at[s, 0:2, yr, sib], ss, rr, 10, SIB)
-        arrived(v.at[s, 0:2, yo, sib], ss, rr, 11, SIB)
-        arrived(v.at[s, 2:4, yo, sib], ss, rr, 12, SIB)
-        full_product(L10, 0, acc)
-
-    gather_first()
+    gather(
+        0, L10,
+        start=do(relay, L10),
+        near=in_turn(do(relay_far, L10), do(own_later, U01)),
+        ready=do(complete, L10),
+    )
     for d in (1, 3, 2):
         arrived(b1g.at[(x + 4 - d) % 4], bsend, brecv, d, ((x + 4 - d) % 4, y, k, z))
 
-    def residual(s, values):
-        v[s, :, y, k] = values.astype(jnp.bfloat16).reshape(4, rows, cols)
-
     residual(1, b1g[...].reshape(own, cols) - acc[...])
-
-    def middle_1():
-        relay_far(LI1)
-        relay(U01)
-        own_send(LI0)
-        complete(LI1)
-
-    gather(1, LI1, middle=middle_1, late=lambda: relay_far(U01))
+    gather(
+        1, LI1,
+        start=in_turn(do(relay, LI1), do(own_later, LI0)),
+        second=in_turn(do(relay_far, LI1), do(own_later, UI1)),
+        far=do(relay, U01),
+        ready=do(complete, LI1),
+    )
 
     residual(2, acc[...])
-
-    def early_2():
-        relay(LI0)
-        own_send(UI1)
-        complete(U01)
-
-    def middle_2():
-        relay_far(LI0)
-        relay(UI1)
-        own_send(UI0)
-
-    def late_2():
-        complete(LI0)
-        full_product(LI0, 0, y0)
-        relay_far(UI1)
-
-    gather(2, U01, early=early_2, middle=middle_2, late=late_2)
+    gather(
+        2, U01,
+        start=do(relay_far, U01),
+        near=in_turn(do(relay, LI0), do(own_later, UI0)),
+        second=do(complete, U01),
+        far=in_turn(do(relay_far, LI0), do(complete, LI0), do(full_product, LI0, 0, y0)),
+    )
 
     residual(3, y0[...] - acc[...])
 
-    def early_3():
-        relay(UI0)
-
-    def middle_3():
+    def other_result():
         complete(UI1)
-        full_product(UI1, 2, acc)
-        result(1)
-        relay_far(UI0)
-        complete(UI0)
-
-    gather(3, UI0, early=early_3, middle=middle_3)
-    result(0)
+        full_product(UI1, 2, y0)
+        result(1, y0)
+
+    gather(
+        3, UI0,
+        start=do(relay, UI1),
+        near=do(relay_far, UI1),
+        second=do(relay, UI0),
+        far=do(relay_far, UI0),
+        ready=in_turn(other_result, do(complete, UI0)),
+    )
+    result(0, acc)
     write(1)
     write(0)
     for c in sent:
@@ -320,7 +312,7 @@
             dma((2, 4)), dma((2, 4)),
         ],
         compiler_params=pltpu.CompilerParams(
-            collective_id=0, has_side_effects=True, vmem_limit_bytes=48 * 2**20
+            collective_id=0, has_side_effects=True, vmem_limit_bytes=53 * 2**20
         ),
     )(split(lower_coupling), split(lower_inverse), split(upper_coupling), split(upper_inverse), right_side)
 

time: 78 us -> 70.7 us (0.906)
  the two profiles are of different devices: /device:TPU:1 before, /device:TPU:8 now
where the time goes in v2:
time: 70.7 us; the launch traced here: 70.6 us
  Pallas kernels  69.8 us (99%)
  local copies, waits for them, and re-layouts  0.8 us (1%)
    pallas_call x1, Pallas kernels, shards(): pl.pallas_call(functools.partial(kernel, depth_z), out_shape=jax.ShapeDty...  69.8 us

profile of v2, /device:TPU:8, one launch (start us, length us, event | category | flops | bytes accessed | tf_op | source)
XLA Modules:
  0.0 70.6 jit_solution(217349589450150431)
XLA Ops:
  0.0 69.8 %shard_map.55 = f32[2,64,1024]{2,1,0:T(8,128)S(1)} custom-call(bf16[2,2,2,16,4096]{4,3,2,1,0:T(8,128)(2,1)} %bitcast.4, bf16[2,2,2,16,2048]{4,3,2,1,0:T(8,128)(2,1)} %bitcast.6, bf16[2,2,2,16,4096]{4,3,2,1,0:T(8,128)(2,1)} %bitcast.5, bf16[2,2,2,16,2048]{4,3,2,1,0:T(8,128)(2,1)} %bitcast.7, f32[2,64,1024]{2,1,0:T(8,128)} %b.1), custom_call_target="tpu_custom_call" | custom-call | tf_op jit(solution)/shard_map/pallas_call | solution.py:292
  69.8 0.8 %copy.7 = f32[2,64,1024]{2,1,0:T(8,128)} copy(f32[2,64,1024]{2,1,0:T(8,128)S(1)} %shard_map.55) | data formatting | bytes 1048576

commit v3 on v0

v3 whole, which is shorter than its diff:
```python
import functools

import jax
import jax.numpy as jnp
from jax import lax
from jax.experimental import pallas as pl
from jax.experimental.pallas import tpu as pltpu
from jax.sharding import Mesh
from jax.sharding import PartitionSpec as P

BLK = ("blk_0", "blk_1", "blk_2")
L10, LI1, U01, LI0, UI1, UI0 = range(6)
CHUNKS = 2


def kernel(
    lc, li, uc, ui, b, o,
    w, v, bv, fst, b1g, y0, ob, ro,
    hsem, vsend, vrecv, msend, mrecv, asend, arecv, bsend, brecv, xsend, xrecv,
):
    rows, width = fst.shape[3], fst.shape[4]
    cols = CHUNKS * width
    own = 4 * rows
    x, y, k, z = (lax.axis_index(a) for a in BLK + ("rhs",))
    t = x // 2
    j = t * (3 - x) + (1 - t) * x
    i = 1 - j
    u = 1 - t
    n = 1 - k
    yr, yl, yo = (y + 1) % 4, (y + 3) % 4, (y + 2) % 4
    SIDE = (x + 1 - 2 * (x % 2), y, k, z)
    PAIR, CROSS, SIB = (3 - x, y, k, z), (3 - x, y, n, z), (x, y, n, z)
    UP, DOWN, FAR = (x, yr, k, z), (x, yl, k, z), (x, yo, k, z)

    def remote(src, dst, ssem, rsem, dev):
        return pltpu.make_async_remote_copy(
            src_ref=src, dst_ref=dst, send_sem=ssem, recv_sem=rsem,
            device_id=dev, device_id_type=pl.DeviceIdType.MESH,
        )

    sent = []

    def send(src, sends, recvs, dev, dst=None):
        c = remote(src, src if dst is None else dst, sends, recvs, dev)
        c.start()
        sent.append(c)

    def arrived(ref, sends, recvs, dev):
        remote(ref, ref, sends, recvs, dev).wait_recv()

    barrier = pltpu.get_barrier_semaphore()
    greeted = [SIDE, PAIR, CROSS, SIB, UP, DOWN, FAR]
    for dev in greeted:
        pl.semaphore_signal(barrier, inc=1, device_id=dev, device_id_type=pl.DeviceIdType.MESH)

    def load_b(s, half, core):
        first = (half * 2 + core) * cols
        return pltpu.make_async_copy(
            b.at[s, :, first:first + cols], bv.at[s, half, core], hsem.at[s, half * 2 + core]
        )

    loads_b = [[load_b(s, half, core) for half in range(2) for core in range(2)] for s in range(2)]
    sep = 32 * rows
    source = [
        lc.at[1, :, 0:sep], li.at[1], uc.at[0, :, sep:2 * sep], li.at[0], ui.at[1], ui.at[0],
    ]
    loads_w = [
        pltpu.make_async_copy(source[m], w.at[m, t, k], hsem.at[2 + m // 4, m % 4]) for m in range(6)
    ]
    for c in loads_b[0]:
        c.start()
    loads_w[0].start()
    for c in loads_b[1]:
        c.start()
    for c in loads_w[1:]:
        c.start()
    for half in range(2):
        for core in range(2):
            loads_b[0][half * 2 + core].wait()
            for c in range(CHUNKS):
                fst[half, core, c] = bv[0, half, core, :, c * width:(c + 1) * width].astype(jnp.bfloat16)
    for c in range(CHUNKS):
        v[0, c, j, t, y, k] = fst[t, k, c]

    pl.semaphore_wait(barrier, len(greeted))

    def own_send(m):
        loads_w[m].wait()
        send(w.at[m, t, k], msend.at[m, 0], mrecv.at[m, 0], PAIR)
        send(w.at[m, t, k], msend.at[m, 1], mrecv.at[m, 1], SIB)

    def pass_on(m):
        arrived(w.at[m, u, k], msend.at[m, 0], mrecv.at[m, 0], PAIR)
        send(w.at[m, u, k], msend.at[m, 2], mrecv.at[m, 2], SIB)

    def complete(m):
        arrived(w.at[m, t, n], msend.at[m, 1], mrecv.at[m, 1], SIB)
        arrived(w.at[m, u, n], msend.at[m, 2], mrecv.at[m, 2], SIB)

    def product(m, s, c):
        total = None
        for jj in range(2):
            for h in range(2):
                first = (jj if h == 0 else 3 - jj) * 8 * rows
                lhs = w[m, :, :, :, first:first + 8 * rows].reshape(own, 8 * rows)
                rhs = v[s, c, jj, h].reshape(8 * rows, width)
                part = jnp.dot(lhs, rhs, preferred_element_type=jnp.float32)
                total = part if total is None else total + part
        return total

    def spread(s, c):
        ss, rr = vsend.at[s, c], vrecv.at[s, c]
        mine = v.at[s, c, j, :, y]
        send(mine, ss.at[0], rr.at[0], FAR)
        send(mine, ss.at[1], rr.at[1], SIDE)
        send(mine, ss.at[2], rr.at[2], UP)
        send(mine, ss.at[3], rr.at[3], DOWN)

    def relay(s, c):
        ss, rr = vsend.at[s, c], vrecv.at[s, c]
        side, far = v.at[s, c, i, :, y], v.at[s, c, j, :, yo]
        arrived(side, ss.at[1], rr.at[1], SIDE)
        send(side, ss.at[5], rr.at[5], UP)
        send(side, ss.at[6], rr.at[6], DOWN)
        arrived(far, ss.at[0], rr.at[0], FAR)
        send(far, ss.at[4], rr.at[4], SIDE)

    def gathered(s, c):
        ss, rr = vsend.at[s, c], vrecv.at[s, c]
        arrived(v.at[s, c, j, :, yl], ss.at[2], rr.at[2], DOWN)
        arrived(v.at[s, c, j, :, yr], ss.at[3], rr.at[3], UP)
        arrived(v.at[s, c, i, :, yl], ss.at[5], rr.at[5], DOWN)
        arrived(v.at[s, c, i, :, yr], ss.at[6], rr.at[6], UP)
        arrived(v.at[s, c, i, :, yo], ss.at[4], rr.at[4], SIDE)

    def residual(s, c, values):
        v[s, c, j, :, y] = values.astype(jnp.bfloat16).reshape(2, 2, rows, width)
        spread(s, c)

    def result(s, c, total):
        ob[s, c] = total.astype(jnp.bfloat16).reshape(2, 2, rows, width)
        ss, rr = xsend.at[s, c], xrecv.at[s, c]
        send(ob.at[s, c, u, k], ss.at[0], rr.at[0], PAIR, ro.at[s, c, t, k])
        send(ob.at[s, c, u, n], ss.at[1], rr.at[1], CROSS, ro.at[s, c, t, k])
        send(ob.at[s, c, t, n], ss.at[2], rr.at[2], SIB, ro.at[s, c, t, k])
        ro[s, c, t, k] = ob[s, c, t, k]

    def write(s, c):
        ss, rr = xsend.at[s, c], xrecv.at[s, c]
        arrived(ro.at[s, c, t, n], ss.at[2], rr.at[2], SIB)
        arrived(ro.at[s, c, u, k], ss.at[0], rr.at[0], PAIR)
        arrived(ro.at[s, c, u, n], ss.at[1], rr.at[1], CROSS)
        for half in range(2):
            for core in range(2):
                first = (half * 2 + core) * cols + c * width
                o[s, :, first:first + width] = ro[s, c, half, core].astype(jnp.float32)

    every = range(CHUNKS)
    for c in every:
        send(fst.at[u, k, c], asend.at[c, 0], arecv.at[c, 0], PAIR, v.at[0, c, j, t, y, k])
        send(fst.at[u, n, c], asend.at[c, 1], arecv.at[c, 1], CROSS, v.at[0, c, j, t, y, k])
        send(fst.at[t, n, c], asend.at[c, 2], arecv.at[c, 2], SIB, v.at[0, c, j, t, y, k])
    own_send(L10)
    for c in loads_b[1]:
        c.wait()
    send(bv.at[1, u, k], bsend.at[0], brecv.at[0], PAIR, b1g.at[t, k])
    send(bv.at[1, u, n], bsend.at[1], brecv.at[1], CROSS, b1g.at[t, k])
    send(bv.at[1, t, n], bsend.at[2], brecv.at[2], SIB, b1g.at[t, k])
    for m in range(1, 6):
        own_send(m)
    b1g[t, k] = bv[1, t, k]
    for c in every:
        arrived(v.at[0, c, j, t, y, n], asend.at[c, 2], arecv.at[c, 2], SIB)
        arrived(v.at[0, c, j, u, y, k], asend.at[c, 0], arecv.at[c, 0], PAIR)
        arrived(v.at[0, c, j, u, y, n], asend.at[c, 1], arecv.at[c, 1], CROSS)
        spread(0, c)
    for c in every:
        relay(0, c)
    pass_on(L10)
    arrived(b1g.at[t, n], bsend.at[2], brecv.at[2], SIB)
    arrived(b1g.at[u, k], bsend.at[0], brecv.at[0], PAIR)
    arrived(b1g.at[u, n], bsend.at[1], brecv.at[1], CROSS)
    complete(L10)
    for c in every:
        gathered(0, c)
        start = b1g[:, :, :, c * width:(c + 1) * width].reshape(own, width)
        residual(1, c, start - product(L10, 0, c))
    for c in every:
        relay(1, c)
    pass_on(LI1)
    complete(LI1)
    for c in every:
        gathered(1, c)
        residual(2, c, product(LI1, 1, c))
    pass_on(U01)
    for c in every:
        relay(2, c)
    complete(U01)
    pass_on(LI0)
    complete(LI0)
    for c in every:
        y0[c] = product(LI0, 0, c)
    for c in every:
        gathered(2, c)
        residual(3, c, y0[c] - product(U01, 2, c))
    pass_on(UI1)
    for c in every:
        relay(3, c)
    complete(UI1)
    for c in every:
        result(1, c, product(UI1, 2, c))
    pass_on(UI0)
    complete(UI0)
    for c in every:
        gathered(3, c)
        result(0, c, product(UI0, 3, c))
    for s in (1, 0):
        for c in every:
            write(s, c)
    for c in sent:
        c.wait_send()


def shards(lower_coupling, upper_coupling, lower_inverse, upper_inverse, right_side):
    rows = right_side.shape[1]
    cols = right_side.shape[2] // 4
    width = cols // CHUNKS
    f32, bf16 = jnp.float32, jnp.bfloat16
    dma = pltpu.SemaphoreType.DMA
    hbm = pl.BlockSpec(memory_space=pltpu.MemorySpace.HBM)
    return pl.pallas_call(
        kernel,
        out_shape=jax.ShapeDtypeStruct(right_side.shape, f32),
        in_specs=[hbm] * 5,
        out_specs=pl.BlockSpec(memory_space=pltpu.MemorySpace.VMEM),
        scratch_shapes=[
            pltpu.VMEM((6, 2, 2, rows, 32 * rows), bf16),
            pltpu.VMEM((4, CHUNKS, 2, 2, 4, 2, rows, width), bf16),
            pltpu.VMEM((2, 2, 2, rows, cols), f32),
            pltpu.VMEM((2, 2, CHUNKS, rows, width), bf16),
            pltpu.VMEM((2, 2, rows, cols), f32),
            pltpu.VMEM((CHUNKS, 4 * rows, width), f32),
            pltpu.VMEM((2, CHUNKS, 2, 2, rows, width), bf16),
            pltpu.VMEM((2, CHUNKS, 2, 2, rows, width), bf16),
            dma((4, 4)),
            dma((4, CHUNKS, 7)), dma((4, CHUNKS, 7)),
            dma((6, 3)), dma((6, 3)),
            dma((CHUNKS, 3)), dma((CHUNKS, 3)),
            dma((3,)), dma((3,)),
            dma((2, CHUNKS, 3)), dma((2, CHUNKS, 3)),
        ],
        compiler_params=pltpu.CompilerParams(
            collective_id=0, has_side_effects=True, vmem_limit_bytes=53 * 2**20
        ),
    )(lower_coupling, lower_inverse, upper_coupling, upper_inverse, right_side)


def solution(mesh):
    finer = Mesh(mesh.devices.reshape(4, 4, 2, mesh.shape["rhs"]), BLK + ("rhs",))
    spec = P(None, BLK, None)
    return jax.shard_map(
        shards,
        mesh=finer,
        in_specs=(spec, spec, spec, spec, P(None, BLK, "rhs")),
        out_specs=P(None, BLK, "rhs"),
        check_vma=False,
    )
```

time: 187 us -> 60.3 us (0.32)
  blocking collectives: 100 us -> 0 us
  Pallas kernels: 0 us -> 59.3 us
  waiting for transfers between devices: 52.3 us -> 0 us
  matrix products: 11.6 us -> 0 us
  local copies, waits for them, and re-layouts: 12.3 us -> 0.8 us
  starting transfers between devices: 8.46 us -> 0 us
    all_to_all x6 -> x0, blocking collectives: 100 us -> none  [from_everyone(): lax.all_to_all(jnp.broadcast_to(array[None], (size, *array.shape)), axis,...]
    pallas_call x0 -> x1, Pallas kernels: none -> 59.3 us  [shards(): pl.pallas_call(kernel, out_shape=jax.ShapeDtypeStruct(right_side.shape, f...]
    all_to_all x2 -> x0, waiting for transfers between devices: 52.3 us -> none  [from_everyone(): lax.all_to_all(jnp.broadcast_to(array[None], (size, *array.shape)), axis,...]
    dot_general x6 -> x0, matrix products: 11.6 us -> none  [the longest x4 7.76 us: sweep(): result = jnp.dot(own_inverse, gathered, preferred_element_type=jnp.float32)]
    all_to_all x2 -> x0, starting transfers between devices: 8.46 us -> none  [from_everyone(): lax.all_to_all(jnp.broadcast_to(array[None], (size, *array.shape)), axis,...]
    broadcast_in_dim x9 -> x0, local copies, waits for them, and re-layouts: 6.93 us -> none  [from_everyone(): jnp.broadcast_to(array[None], (size, *array.shape))]
    all_to_all x4 -> x0, local copies, waits for them, and re-layouts: 2.81 us -> none  [from_everyone(): lax.all_to_all(jnp.broadcast_to(array[None], (size, *array.shape)), axis,...]
  transfers between devices with their start and end apart: 2 -> 0, of which waited for: 2 -> 0; matrix products, arithmetic and copies ran while one was open for 3% -> 0% of each run, Pallas kernels for 0% -> 0%
where the time goes in v3:
time: 60.3 us; the launch traced here: 60.1 us
  Pallas kernels  59.3 us (98%)
  local copies, waits for them, and re-layouts  0.8 us (1%)
    pallas_call x1, Pallas kernels, shards(): pl.pallas_call(kernel, out_shape=jax.ShapeDtypeStruct(right_side.shape, f...  59.3 us

profile of v3, /device:TPU:1, one launch (start us, length us, event | category | flops | bytes accessed | tf_op | source)
XLA Modules:
  0.0 60.1 jit_solution(5179277785683140321)
XLA Ops:
  0.0 59.3 %shard_map.55 = f32[2,64,1024]{2,1,0:T(8,128)S(1)} custom-call(bf16[2,64,4096]{2,1,0:T(8,128)(2,1)} %lc.1, bf16[2,64,2048]{2,1,0:T(8,128)(2,1)} %li.1, bf16[2,64,4096]{2,1,0:T(8,128)(2,1)} %uc.1, bf16[2,64,2048]{2,1,0:T(8,128)(2,1)} %ui.1, f32[2,64,1024]{2,1,0:T(8,128)} %b.1), custom_call_target="tpu_custom_call" | custom-call | tf_op jit(solution)/shard_map/pallas_call | solution.py:231
  59.3 0.8 %copy.7 = f32[2,64,1024]{2,1,0:T(8,128)} copy(f32[2,64,1024]{2,1,0:T(8,128)S(1)} %shard_map.55) | data formatting | bytes 1048576

commit v4 on v3

v4 whole, which is shorter than its diff:
```python
import functools

import jax
import jax.numpy as jnp
from jax import lax
from jax.experimental import pallas as pl
from jax.experimental.pallas import tpu as pltpu
from jax.sharding import Mesh
from jax.sharding import PartitionSpec as P

BLK = ("blk_0", "blk_1", "blk_2")
L10, LI1, LI0, U01, UI1, UI0 = range(6)
CHUNKS = 2


def kernel(
    lc, li, uc, ui, b, o,
    w, v, bv, fst, b1g, y0, ob, ro,
    hsem, vsend, vrecv, msend, mrecv, asend, arecv, bsend, brecv, xsend, xrecv,
):
    rows, width = fst.shape[3], fst.shape[4]
    cols = CHUNKS * width
    own = 4 * rows
    x, y, k, z = (lax.axis_index(a) for a in BLK + ("rhs",))
    t = x // 2
    j = t * (3 - x) + (1 - t) * x
    i = 1 - j
    u = 1 - t
    n = 1 - k
    yr, yl, yo = (y + 1) % 4, (y + 3) % 4, (y + 2) % 4
    SIDE = (x + 1 - 2 * (x % 2), y, k, z)
    PAIR, CROSS, SIB = (3 - x, y, k, z), (3 - x, y, n, z), (x, y, n, z)
    UP, DOWN, FAR = (x, yr, k, z), (x, yl, k, z), (x, yo, k, z)

    def remote(src, dst, ssem, rsem, dev):
        return pltpu.make_async_remote_copy(
            src_ref=src, dst_ref=dst, send_sem=ssem, recv_sem=rsem,
            device_id=dev, device_id_type=pl.DeviceIdType.MESH,
        )

    sent = []

    def send(src, sends, recvs, dev, dst=None):
        c = remote(src, src if dst is None else dst, sends, recvs, dev)
        c.start()
        sent.append(c)

    def arrived(ref, sends, recvs, dev):
        remote(ref, ref, sends, recvs, dev).wait_recv()

    barrier = pltpu.get_barrier_semaphore()
    greeted = [SIDE, PAIR, CROSS, SIB, UP, DOWN, FAR]
    for dev in greeted:
        pl.semaphore_signal(barrier, inc=1, device_id=dev, device_id_type=pl.DeviceIdType.MESH)

    def load_b(s, half, core, c):
        first = (half * 2 + core) * cols + c * width
        return pltpu.make_async_copy(
            b.at[s, :, first:first + width], bv.at[s, half, core, c],
            hsem.at[s, (half * 2 + core) * CHUNKS + c],
        )

    pieces = [(half, core, c) for half in range(2) for core in range(2) for c in range(CHUNKS)]
    loads_b = [[load_b(s, *piece) for piece in pieces] for s in range(2)]
    sep = 32 * rows
    source = [
        lc.at[1, :, 0:sep], li.at[1], li.at[0], uc.at[0, :, sep:2 * sep], ui.at[1], ui.at[0],
    ]
    loads_w = [
        pltpu.make_async_copy(source[m], w.at[m, t, k], hsem.at[2, m]) for m in range(6)
    ]
    for c in loads_b[0]:
        c.start()
    loads_w[0].start()
    for c in loads_b[1]:
        c.start()
    for c in loads_w[1:]:
        c.start()
    for piece, load in zip(pieces, loads_b[0]):
        load.wait()
        fst[piece] = bv[(0,) + piece].astype(jnp.bfloat16)
    for c in range(CHUNKS):
        v[0, c, j, t, y, k] = fst[t, k, c]

    pl.semaphore_wait(barrier, len(greeted))

    def own_send(m):
        loads_w[m].wait()
        send(w.at[m, t, k], msend.at[m, 0], mrecv.at[m, 0], PAIR)
        send(w.at[m, t, k], msend.at[m, 1], mrecv.at[m, 1], SIB)

    def pass_on(m):
        arrived(w.at[m, u, k], msend.at[m, 0], mrecv.at[m, 0], PAIR)
        send(w.at[m, u, k], msend.at[m, 2], mrecv.at[m, 2], SIB)

    def own_complete(m):
        arrived(w.at[m, t, n], msend.at[m, 1], mrecv.at[m, 1], SIB)

    def pair_complete(m):
        arrived(w.at[m, u, n], msend.at[m, 2], mrecv.at[m, 2], SIB)

    def complete(m):
        own_complete(m)
        pair_complete(m)

    def rows_of(chip, m, s, c):
        total = None
        for jj in range(2):
            for h in range(2):
                first = (jj if h == 0 else 3 - jj) * 8 * rows
                lhs = w[m, chip, :, :, first:first + 8 * rows]
                rhs = v[s, c, jj, h].reshape(8 * rows, width)
                part = jnp.dot(lhs.reshape(-1, 8 * rows), rhs, preferred_element_type=jnp.float32)
                total = part if total is None else total + part
        return total

    def product(m, s, c):
        return rows_of(slice(None), m, s, c)

    def near(s, c, e, h):
        ss, rr = vsend.at[s, c], vrecv.at[s, c]
        send(v.at[s, c, j, h, y], ss.at[2, e], rr.at[2, e], UP)
        send(v.at[s, c, j, h, y], ss.at[3, e], rr.at[3, e], DOWN)

    def spread(s, c, halves):
        ss, rr = vsend.at[s, c], vrecv.at[s, c]
        for e, h in halves:
            send(v.at[s, c, j, h, y], ss.at[0, e], rr.at[0, e], FAR)
            send(v.at[s, c, j, h, y], ss.at[1, e], rr.at[1, e], SIDE)
        if halves[0][0] == 0:
            near(s, c, *halves[0])

    def relay(s, c, halves):
        ss, rr = vsend.at[s, c], vrecv.at[s, c]
        for e, h in halves:
            side = v.at[s, c, i, h, y]
            arrived(side, ss.at[1, e], rr.at[1, e], SIDE)
            if e == 0:
                near(s, c, *halves[1])
            send(side, ss.at[5, e], rr.at[5, e], UP)
            send(side, ss.at[6, e], rr.at[6, e], DOWN)
        for e, h in halves:
            far = v.at[s, c, j, h, yo]
            arrived(far, ss.at[0, e], rr.at[0, e], FAR)
            send(far, ss.at[4, e], rr.at[4, e], SIDE)

    def gathered(s, c, halves):
        ss, rr = vsend.at[s, c], vrecv.at[s, c]
        for e, h in halves:
            arrived(v.at[s, c, j, h, yl], ss.at[2, e], rr.at[2, e], DOWN)
            arrived(v.at[s, c, i, h, yl], ss.at[5, e], rr.at[5, e], DOWN)
            arrived(v.at[s, c, j, h, yr], ss.at[3, e], rr.at[3, e], UP)
            arrived(v.at[s, c, i, h, yr], ss.at[6, e], rr.at[6, e], UP)
            arrived(v.at[s, c, i, h, yo], ss.at[4, e], rr.at[4, e], SIDE)

    def residual(s, c, values):
        v[s, c, j, :, y] = values.astype(jnp.bfloat16).reshape(2, 2, rows, width)
        spread(s, c, plain)

    def result_own(s, c, total):
        ob[s, c, t] = total.astype(jnp.bfloat16).reshape(2, rows, width)
        send(ob.at[s, c, t, n], xsend.at[s, c, 2], xrecv.at[s, c, 2], SIB, ro.at[s, c, t, k])
        ro[s, c, t, k] = ob[s, c, t, k]

    def result_pair(s, c, total):
        ob[s, c, u] = total.astype(jnp.bfloat16).reshape(2, rows, width)
        send(ob.at[s, c, u, k], xsend.at[s, c, 0], xrecv.at[s, c, 0], PAIR, ro.at[s, c, t, k])
        send(ob.at[s, c, u, n], xsend.at[s, c, 1], xrecv.at[s, c, 1], CROSS, ro.at[s, c, t, k])

    def write(s, c):
        ss, rr = xsend.at[s, c], xrecv.at[s, c]
        arrived(ro.at[s, c, t, n], ss.at[2], rr.at[2], SIB)
        arrived(ro.at[s, c, u, k], ss.at[0], rr.at[0], PAIR)
        arrived(ro.at[s, c, u, n], ss.at[1], rr.at[1], CROSS)
        for half in range(2):
            for core in range(2):
                first = (half * 2 + core) * cols + c * width
                o[s, :, first:first + width] = ro[s, c, half, core].astype(jnp.float32)

    every = range(CHUNKS)

    def relays(s, halves):
        for c in every:
            relay(s, c, halves)

    for c in every:
        send(fst.at[u, k, c], asend.at[c, 0], arecv.at[c, 0], PAIR, v.at[0, c, j, t, y, k])
        send(fst.at[u, n, c], asend.at[c, 1], arecv.at[c, 1], CROSS, v.at[0, c, j, t, y, k])
        send(fst.at[t, n, c], asend.at[c, 2], arecv.at[c, 2], SIB, v.at[0, c, j, t, y, k])
    own_send(L10)
    for c in loads_b[1]:
        c.wait()
    for c in every:
        send(bv.at[1, u, k, c], bsend.at[c, 0], brecv.at[c, 0], PAIR, b1g.at[c, t, k])
        send(bv.at[1, u, n, c], bsend.at[c, 1], brecv.at[c, 1], CROSS, b1g.at[c, t, k])
        send(bv.at[1, t, n, c], bsend.at[c, 2], brecv.at[c, 2], SIB, b1g.at[c, t, k])
    for m in range(1, 6):
        own_send(m)
    for c in every:
        b1g[c, t, k] = bv[1, t, k, c]
    plain, mine_first = ((0, 0), (1, 1)), ((0, t), (1, u))
    for c in every:
        arrived(v.at[0, c, j, t, y, n], asend.at[c, 2], arecv.at[c, 2], SIB)
        spread(0, c, mine_first[:1])
    for c in every:
        arrived(v.at[0, c, j, u, y, k], asend.at[c, 0], arecv.at[c, 0], PAIR)
        arrived(v.at[0, c, j, u, y, n], asend.at[c, 1], arecv.at[c, 1], CROSS)
        spread(0, c, mine_first[1:])
    relays(0, mine_first)
    pass_on(L10)
    complete(L10)
    for c in every:
        gathered(0, c, mine_first)
        arrived(b1g.at[c, t, n], bsend.at[c, 2], brecv.at[c, 2], SIB)
        arrived(b1g.at[c, u, k], bsend.at[c, 0], brecv.at[c, 0], PAIR)
        arrived(b1g.at[c, u, n], bsend.at[c, 1], brecv.at[c, 1], CROSS)
        start = b1g[c].reshape(own, width)
        residual(1, c, start - product(L10, 0, c))
    relays(1, plain)
    pass_on(LI1)
    complete(LI1)
    for c in every:
        gathered(1, c, plain)
        residual(2, c, product(LI1, 1, c))
    pass_on(LI0)
    relays(2, plain)
    complete(LI0)
    pass_on(U01)
    for c in every:
        y0[c] = product(LI0, 0, c)
    complete(U01)
    for c in every:
        gathered(2, c, plain)
        residual(3, c, y0[c] - product(U01, 2, c))
    pass_on(UI1)
    relays(3, plain)
    own_complete(UI1)
    for c in every:
        result_own(1, c, rows_of(t, UI1, 2, c))
    pair_complete(UI1)
    for c in every:
        result_pair(1, c, rows_of(u, UI1, 2, c))
    own_complete(UI0)
    gathered(3, 0, plain)
    result_own(0, 0, rows_of(t, UI0, 3, 0))
    pass_on(UI0)
    gathered(3, 1, plain)
    result_own(0, 1, rows_of(t, UI0, 3, 1))
    pair_complete(UI0)
    for c in every:
        result_pair(0, c, rows_of(u, UI0, 3, c))
    for s in (1, 0):
        for c in every:
            write(s, c)
    for c in sent:
        c.wait_send()


def shards(lower_coupling, upper_coupling, lower_inverse, upper_inverse, right_side):
    rows = right_side.shape[1]
    cols = right_side.shape[2] // 4
    width = cols // CHUNKS
    f32, bf16 = jnp.float32, jnp.bfloat16
    dma = pltpu.SemaphoreType.DMA
    hbm = pl.BlockSpec(memory_space=pltpu.MemorySpace.HBM)
    return pl.pallas_call(
        kernel,
        out_shape=jax.ShapeDtypeStruct(right_side.shape, f32),
        in_specs=[hbm] * 5,
        out_specs=pl.BlockSpec(memory_space=pltpu.MemorySpace.VMEM),
        scratch_shapes=[
            pltpu.VMEM((6, 2, 2, rows, 32 * rows), bf16),
            pltpu.VMEM((4, CHUNKS, 2, 2, 4, 2, rows, width), bf16),
            pltpu.VMEM((2, 2, 2, CHUNKS, rows, width), f32),
            pltpu.VMEM((2, 2, CHUNKS, rows, width), bf16),
            pltpu.VMEM((CHUNKS, 2, 2, rows, width), f32),
            pltpu.VMEM((CHUNKS, 4 * rows, width), f32),
            pltpu.VMEM((2, CHUNKS, 2, 2, rows, width), bf16),
            pltpu.VMEM((2, CHUNKS, 2, 2, rows, width), bf16),
            dma((3, 8)),
            dma((4, CHUNKS, 7, 2)), dma((4, CHUNKS, 7, 2)),
            dma((6, 3)), dma((6, 3)),
            dma((CHUNKS, 3)), dma((CHUNKS, 3)),
            dma((CHUNKS, 3)), dma((CHUNKS, 3)),
            dma((2, CHUNKS, 3)), dma((2, CHUNKS, 3)),
        ],
        compiler_params=pltpu.CompilerParams(
            collective_id=0, has_side_effects=True, vmem_limit_bytes=53 * 2**20
        ),
    )(lower_coupling, lower_inverse, upper_coupling, upper_inverse, right_side)


def solution(mesh):
    finer = Mesh(mesh.devices.reshape(4, 4, 2, mesh.shape["rhs"]), BLK + ("rhs",))
    spec = P(None, BLK, None)
    return jax.shard_map(
        shards,
        mesh=finer,
        in_specs=(spec, spec, spec, spec, P(None, BLK, "rhs")),
        out_specs=P(None, BLK, "rhs"),
        check_vma=False,
    )
```

time: 60.3 us -> 59.8 us (level)
  no operation moved by 1% of the time
where the time goes in v4:
time: 59.8 us; the launch traced here: 59.7 us
  Pallas kernels  58.9 us (98%)
  local copies, waits for them, and re-layouts  0.8 us (1%)
    pallas_call x1, Pallas kernels, shards(): pl.pallas_call(kernel, out_shape=jax.ShapeDtypeStruct(right_side.shape, f...  58.9 us

profile of v4, /device:TPU:1, one launch (start us, length us, event | category | flops | bytes accessed | tf_op | source)
XLA Modules:
  0.0 59.7 jit_solution(8155863877975004463)
XLA Ops:
  0.0 58.9 %shard_map.55 = f32[2,64,1024]{2,1,0:T(8,128)S(1)} custom-call(bf16[2,64,4096]{2,1,0:T(8,128)(2,1)} %lc.1, bf16[2,64,2048]{2,1,0:T(8,128)(2,1)} %li.1, bf16[2,64,4096]{2,1,0:T(8,128)(2,1)} %uc.1, bf16[2,64,2048]{2,1,0:T(8,128)(2,1)} %ui.1, f32[2,64,1024]{2,1,0:T(8,128)} %b.1), custom_call_target="tpu_custom_call" | custom-call | tf_op jit(solution)/shard_map/pallas_call | solution.py:266
  58.9 0.8 %copy.7 = f32[2,64,1024]{2,1,0:T(8,128)} copy(f32[2,64,1024]{2,1,0:T(8,128)S(1)} %shard_map.55) | data formatting | bytes 1048576

commit v5 on v4

--- a/solution.py
+++ b/solution.py
@@ -22,14 +22,15 @@
     cols = CHUNKS * width
     own = 4 * rows
     x, y, k, z = (lax.axis_index(a) for a in BLK + ("rhs",))
-    t = x // 2
-    j = t * (3 - x) + (1 - t) * x
+    t = ((x + 1) // 2) % 2
+    j = x // 2
     i = 1 - j
     u = 1 - t
     n = 1 - k
     yr, yl, yo = (y + 1) % 4, (y + 3) % 4, (y + 2) % 4
-    SIDE = (x + 1 - 2 * (x % 2), y, k, z)
-    PAIR, CROSS, SIB = (3 - x, y, k, z), (3 - x, y, n, z), (x, y, n, z)
+    xp = x + 1 - 2 * (x % 2)
+    SIDE = (3 - x, y, k, z)
+    PAIR, CROSS, SIB = (xp, y, k, z), (xp, y, n, z), (x, y, n, z)
     UP, DOWN, FAR = (x, yr, k, z), (x, yl, k, z), (x, yo, k, z)
 
     def remote(src, dst, ssem, rsem, dev):
@@ -107,7 +108,7 @@
         total = None
         for jj in range(2):
             for h in range(2):
-                first = (jj if h == 0 else 3 - jj) * 8 * rows
+                first = (h if jj == 0 else 3 - h) * 8 * rows
                 lhs = w[m, chip, :, :, first:first + 8 * rows]
                 rhs = v[s, c, jj, h].reshape(8 * rows, width)
                 part = jnp.dot(lhs.reshape(-1, 8 * rows), rhs, preferred_element_type=jnp.float32)

time: 59.8 us -> 58.6 us (0.980)
  Pallas kernels: 58.9 us -> 57.7 us
    pallas_call x1, Pallas kernels: 58.9 us -> 57.7 us  [shards(): pl.pallas_call(kernel, out_shape=jax.ShapeDtypeStruct(right_side.shape, f...]
where the time goes in v5:
time: 58.6 us; the launch traced here: 58.5 us
  Pallas kernels  57.7 us (98%)
  local copies, waits for them, and re-layouts  0.8 us (1%)
    pallas_call x1, Pallas kernels, shards(): pl.pallas_call(kernel, out_shape=jax.ShapeDtypeStruct(right_side.shape, f...  57.7 us

profile of v5, /device:TPU:1, one launch (start us, length us, event | category | flops | bytes accessed | tf_op | source)
XLA Modules:
  0.0 58.5 jit_solution(4098291893657091221)
XLA Ops:
  0.0 57.7 %shard_map.55 = f32[2,64,1024]{2,1,0:T(8,128)S(1)} custom-call(bf16[2,64,4096]{2,1,0:T(8,128)(2,1)} %lc.1, bf16[2,64,2048]{2,1,0:T(8,128)(2,1)} %li.1, bf16[2,64,4096]{2,1,0:T(8,128)(2,1)} %uc.1, bf16[2,64,2048]{2,1,0:T(8,128)(2,1)} %ui.1, f32[2,64,1024]{2,1,0:T(8,128)} %b.1), custom_call_target="tpu_custom_call" | custom-call | tf_op jit(solution)/shard_map/pallas_call | solution.py:267
  57.7 0.8 %copy.7 = f32[2,64,1024]{2,1,0:T(8,128)} copy(f32[2,64,1024]{2,1,0:T(8,128)S(1)} %shard_map.55) | data formatting | bytes 1048576
